TPU v7x, 32 devices: a whole 2x2x4 slice. The times are simulated.
32 devices in a mesh: dp: 8 (over y, x, core), seq: 4 (over z).
Axes of the slice: x: 2, y: 2, z: 4, core: 2. Of those that a mesh axis runs over, the one named last changes fastest.
Arguments:
- hidden_in: bfloat16 [8, 512, 2048], P('dp', 'seq'), may hold values from -6 to 6
- cotangent: bfloat16 [8, 512, 2048], P('dp', 'seq'), may hold values from -6 to 6
- norm_gain: float32 [2048], P('dp'), may hold values from 0.1 to 1.9
- route_weights: float32 [8, 512, 10], P('dp', 'seq'), may hold values from 0.1 to 1
- expert_ids: int32 [8, 512, 10], P('dp', 'seq'), may hold values from 0 to 63, all different within a row; in each aligned block of 128 rows (0 to 127, 128 to 255, ..., all dimensions but the last counted through in order) at most 24 rows name the same one
- expert_gate: bfloat16 [64, 2048, 512], P(('dp', 'seq')), may hold values from -0.125 to 0.125
- expert_up: bfloat16 [64, 2048, 512], P(('dp', 'seq')), may hold values from -0.125 to 0.125
- expert_down: bfloat16 [64, 512, 2048], P(('dp', 'seq')), may hold values from -0.25 to 0.25
Outputs:
- grad_hidden: bfloat16 [8, 512, 2048], P('dp', 'seq')
- grad_gain: float32 [2048], P('dp')
- grad_gate: bfloat16 [64, 2048, 512], P(('dp', 'seq'))
- grad_up: bfloat16 [64, 2048, 512], P(('dp', 'seq'))
- grad_down: bfloat16 [64, 512, 2048], P(('dp', 'seq'))
Inputs may be any that keep to these rules, and one draw needn't show every extreme that they name: `expert_ids`: each token names 10 different experts. Among the rows of one device no expert is named by more than 24 of them, and in some device one expert is named by exactly 24.
All inputs are finite; a program needn't handle non-finite values.
Results may differ from a plain program's by a relative error of at most 0.0072.
Values may be sent and summed in bfloat16 or wider, within the bound.
No kernel may reach another device: no remote copies, remote signals or barrier semaphores. Data moves between devices by JAX's collectives and lax.ppermute only.
A program may use at most 192 MiB of HBM per device.

v0:
```python
import jax
import jax.numpy as jnp
from jax import lax
from jax.sharding import PartitionSpec as P

TOP = 10
EPSILON = 1e-06


def shards(
    hidden_in, cotangent, norm_gain, route_weights, expert_ids, expert_gate, expert_up, expert_down
):
    tokens_here = hidden_in.shape[1]
    model_width = hidden_in.shape[2]
    local_experts = expert_gate.shape[0]
    dp_count = lax.axis_size("dp")
    seq_count = lax.axis_size("seq")
    devices = dp_count * seq_count
    expert_count = local_experts * devices
    capacity = max(2, tokens_here * TOP * 6 // (5 * expert_count))
    dp_at = lax.axis_index("dp")
    seq_at = lax.axis_index("seq")
    my_index = dp_at * seq_count + seq_at
    upstream = cotangent[0]
    all_grads = lax.all_gather(upstream, ("dp", "seq"), axis=0)
    gain_full = lax.all_gather(norm_gain, "dp", axis=0, tiled=True)
    inputs = hidden_in[0].astype(jnp.float32)
    inverse_root = lax.rsqrt(jnp.mean(inputs * inputs, axis=1, keepdims=True) + EPSILON)
    scaled = inputs * inverse_root
    normed = (scaled * gain_full[None, :]).astype(jnp.bfloat16)
    all_rows = lax.all_gather(normed, ("dp", "seq"), axis=0)
    ids_here = expert_ids[0]
    weights_here = route_weights[0]
    ids_all = lax.all_gather(ids_here.T, ("dp", "seq"), axis=0, tiled=False)
    weights_all = lax.all_gather(weights_here.T, ("dp", "seq"), axis=0, tiled=False)
    place = jnp.arange(tokens_here, dtype=jnp.int32)
    upper = (place[:, None] < place[None, :]).astype(jnp.bfloat16)
    slots = jnp.arange(capacity, dtype=jnp.int32)
    my_experts = my_index * local_experts + jnp.arange(local_experts, dtype=jnp.int32)
    named = ids_all[:, None, :, :] == my_experts[None, :, None, None]
    chosen = jnp.any(named, axis=2)
    weight = jnp.sum(jnp.where(named, weights_all[:, None, :, :], 0.0), axis=2)
    rank = jnp.einsum(
        "nit,tu->niu", chosen.astype(jnp.bfloat16), upper, preferred_element_type=jnp.float32
    ).astype(jnp.int32)
    picks = chosen[:, :, None, :] & (rank[:, :, None, :] == slots[None, None, :, None])
    row_weight = jnp.sum(jnp.where(picks, weight[:, :, None, :], 0.0), axis=3)
    picks = picks.reshape(devices, local_experts * capacity, tokens_here).astype(jnp.bfloat16)
    row_weight = row_weight.reshape(devices, local_experts * capacity, 1)

    def pick(table):
        return jnp.einsum("nst,ntd->nsd", picks, table, preferred_element_type=jnp.float32)

    four_shape = (devices, local_experts, capacity, model_width)
    rows_grad = (row_weight * pick(all_grads)).astype(jnp.bfloat16).reshape(four_shape)
    rows_in = pick(all_rows).astype(jnp.bfloat16).reshape(four_shape)
    grad_act = jnp.einsum(
        "nicd,ifd->nicf", rows_grad, expert_down, preferred_element_type=jnp.float32
    )
    pre_gate = jnp.einsum(
        "nicd,idf->nicf", rows_in, expert_gate, preferred_element_type=jnp.float32
    )
    pre_up = jnp.einsum("nicd,idf->nicf", rows_in, expert_up, preferred_element_type=jnp.float32)
    sigmoid_gate = jax.nn.sigmoid(pre_gate)
    silu_gate = pre_gate * sigmoid_gate
    activation = (silu_gate * pre_up).astype(jnp.bfloat16)
    gate_back = (grad_act * pre_up * sigmoid_gate * (1.0 + pre_gate * (1.0 - sigmoid_gate))).astype(
        jnp.bfloat16
    )
    up_back = (grad_act * silu_gate).astype(jnp.bfloat16)
    returned = (
        jnp.einsum("nicf,idf->nicd", gate_back, expert_gate, preferred_element_type=jnp.float32)
        + jnp.einsum("nicf,idf->nicd", up_back, expert_up, preferred_element_type=jnp.float32)
    ).astype(jnp.bfloat16)
    back_rows = lax.all_to_all(
        returned.reshape(devices, local_experts * capacity, model_width),
        ("dp", "seq"),
        split_axis=0,
        concat_axis=0,
        tiled=True,
    )
    grad_down = jnp.einsum(
        "nicf,nicd->ifd", activation, rows_grad, preferred_element_type=jnp.float32
    ).astype(jnp.bfloat16)
    grad_gate = jnp.einsum(
        "nicd,nicf->idf", rows_in, gate_back, preferred_element_type=jnp.float32
    ).astype(jnp.bfloat16)
    grad_up = jnp.einsum(
        "nicd,nicf->idf", rows_in, up_back, preferred_element_type=jnp.float32
    ).astype(jnp.bfloat16)
    experts_range = jnp.arange(expert_count, dtype=jnp.int32)
    chosen_here = jnp.any(ids_here[:, :, None] == experts_range[None, None, :], axis=1)
    rank_here = jnp.dot(
        upper.T, chosen_here.astype(jnp.bfloat16), preferred_element_type=jnp.float32
    ).astype(jnp.int32)
    sums = (
        (chosen_here[:, :, None] & (rank_here[:, :, None] == slots[None, None, :]))
        .reshape(tokens_here, expert_count * capacity)
        .astype(jnp.bfloat16)
    )
    summed = jnp.dot(
        sums,
        back_rows.reshape(expert_count * capacity, model_width),
        preferred_element_type=jnp.float32,
    )
    local_gain = jnp.sum(summed * scaled, axis=0)
    total_gain = lax.psum(local_gain, ("dp", "seq"))
    shard_width = norm_gain.shape[0]
    grad_gain = lax.dynamic_slice(total_gain, (dp_at * shard_width,), (shard_width,))
    gained = summed * gain_full[None, :]
    centered = jnp.mean(gained * scaled, axis=1, keepdims=True)
    grad_hidden = (
        upstream.astype(jnp.float32) + inverse_root * (gained - scaled * centered)
    ).astype(jnp.bfloat16)
    return (grad_hidden.reshape(hidden_in.shape), grad_gain, grad_gate, grad_up, grad_down)


def solution(mesh):
    return jax.shard_map(
        shards,
        mesh=mesh,
        in_specs=(
            P("dp", "seq", None),
            P("dp", "seq", None),
            P("dp"),
            P("dp", "seq", None),
            P("dp", "seq", None),
            P(("dp", "seq"), None, None),
            P(("dp", "seq"), None, None),
            P(("dp", "seq"), None, None),
        ),
        out_specs=(
            P("dp", "seq", None),
            P("dp"),
            P(("dp", "seq"), None, None),
            P(("dp", "seq"), None, None),
            P(("dp", "seq"), None, None),
        ),
        check_vma=False,
    )
```

profile of v0, /device:TPU:0, one launch (start us, length us, event | category | flops | bytes accessed | tf_op | source)
XLA Modules:
  0.0 491.8 jit_solution(4126240018301125779)
XLA Ops:
  7.2 0.0 all-gather.10.cloned.1.call-start
  7.2 1.2 fusion.40
  8.5 10.6 %all-gather.4 = f32[8,1,256]{2,1,0:T(1,128)S(1)} all-gather(f32[1,1,256]{2,1,0:T(1,128)} %bitcast.164), channel_id=1, replica_groups=mesh['dp'=8,'seq'=4] {'dp'}, dimensions={0}, use_global_device_ids=true | all-gather | bytes 9216 | tf_op jit(solution)/shard_map/all_gather | solution.py:26
  19.0 0.0 copy-done.11
  19.0 0.6 copy-done.9
  19.6 2.0 fusion.42
  21.6 0.0 all-gather.10.cloned.1.call-update
  21.7 0.0 all-gather.8.cloned.1.call-start
  21.7 0.7 all-gather.8.cloned.1.call-update
  22.4 0.1 eq.88
  22.5 0.7 copy.91
  23.2 0.7 copy.92
  23.9 74.0 %all-gather.3 = f32[32,10,128]{2,1,0:T(8,128)S(1)} all-gather(f32[1,10,128]{2,1,0:T(8,128)S(1)} %bitcast.163), channel_id=3, replica_groups=mesh['dp'=8,'seq'=4] {'dp','seq'}, dimensions={0}, use_global_device_ids=true | all-gather | bytes 168960 | tf_op jit(solution)/shard_map/all_gather | solution.py:35
  97.8 0.1 copy.55
  97.9 69.5 %all-gather.2 = s32[32,10,128]{2,1,0:T(8,128)S(1)} all-gather(s32[1,10,128]{2,1,0:T(8,128)S(1)} %bitcast.161), channel_id=2, replica_groups=mesh['dp'=8,'seq'=4] {'dp','seq'}, dimensions={0}, use_global_device_ids=true | all-gather | bytes 168960 | tf_op jit(solution)/shard_map/all_gather | solution.py:34
  167.4 0.1 copy.52
  167.5 0.1 fusion.47
  167.6 0.1 compare_reduce_fusion
  167.7 0.1 convolution_convert_fusion.1
  167.9 0.4 select_reduce_fusion
  168.3 0.1 copy.57
  168.4 0.1 copy.58
  168.4 0.2 fusion.45
  168.7 0.0 all-gather.10.cloned.1.call-done
  168.7 0.0 copy-start.3
  168.7 8.7 %convolution_convert_fusion = bf16[32,48,2048]{2,1,0:T(8,128)(2,1)S(1)} fusion(pred[32,48,128]{2,1,0:T(8,128)(4,1)S(1)} %fusion.45, bf16[32,128,2048]{2,1,0:T(8,128)(2,1)} %all-gather.10.cloned.1.call-done), kind=kOutput, calls=%fused_computation.14 | convolution fusion | flops 808452096 | bytes 23265280 | tf_op jit(solution)/shard_map/nst,ntd->nsd/dot_general | solution.py:52
  177.4 0.0 copy-start.1
  177.4 0.0 copy-done.3
  177.4 0.0 copy-start.4
  177.4 5.1 %fusion.1 = f32[2,32,24,512]{3,2,1,0:T(8,128)} fusion(bf16[32,2,24,2048]{3,2,1,0:T(8,128)(2,1)S(1)} %bitcast.152, bf16[2,2048,512]{2,1,0:T(8,128)(2,1)S(1)} %copy-done.3), kind=kOutput, calls=%fused_computation.6 | convolution fusion | flops 3221225472 | bytes 13631488 | tf_op jit(solution)/shard_map/nicd,idf->nicf/dot_general | solution.py:60
  182.6 0.0 copy-done.1
  182.6 0.0 copy-done.4
  182.6 5.1 %fusion.3 = f32[2,32,24,512]{3,2,1,0:T(8,128)} fusion(bf16[32,2,24,2048]{3,2,1,0:T(8,128)(2,1)S(1)} %bitcast.153, bf16[2,2048,512]{2,1,0:T(8,128)(2,1)S(1)} %copy-done.4), kind=kOutput, calls=%fused_computation.8 | convolution fusion | flops 3221225472 | bytes 13631488 | tf_op jit(solution)/shard_map/nicd,idf->nicf/dot_general | solution.py:63
  187.7 68.5 %all-gather.8.cloned.1.call-done = bf16[32,128,2048]{2,1,0:T(8,128)(2,1)} async-done(((bf16[1,128,2048]{2,1,0:T(8,128)(2,1)}), bf16[32,128,2048]{2,1,0:T(8,128)(2,1)}) %all-gather.8.cloned.1.call-update) | async-done | bytes 16777232 | tf_op jit(solution)/shard_map/all_gather | solution.py:25
  256.2 8.1 %multiply_convert_fusion = bf16[32,48,2048]{2,1,0:T(8,128)(2,1)S(1)} fusion(f32[32,48]{1,0:T(8,128)S(1)} %copy.58, pred[32,48,128]{2,1,0:T(8,128)(4,1)S(1)} %fusion.45, bf16[32,128,2048]{2,1,0:T(8,128)(2,1)} %all-gather.8.cloned.1.call-done), kind=kOutput, calls=%fused_computation.1 | convolution fusion | flops 811597824 | bytes 23271424 | tf_op jit(solution)/shard_map/nst,ntd->nsd/dot_general | solution.py:52
  264.3 0.0 copy-start
  264.3 9.9 %fusion.25 = (bf16[32,2,24,512]{3,2,0,1:T(8,128)(2,1)S(1)}, bf16[32,2,24,512]{3,2,0,1:T(8,128)(2,1)S(1)}) fusion(f32[2,32,24,512]{3,2,1,0:T(8,128)} %fusion.1, f32[2,32,24,512]{3,2,1,0:T(8,128)} %fusion.3, bf16[2,512,2048]{2,1,0:T(8,128)(2,1)} %param.15, bf16[32,2,24,2048]{3,2,1,0:T(8,128)(2,1)S(1)} %bitcast.148), kind=kOutput, calls=%fused_computation.35 | convolution fusion | flops 3231449088 | bytes 19922944 | tf_op jit(solution)/shard_map/nicd,ifd->nicf/dot_general | solution.py:57
  274.2 0.0 copy-done
  274.2 0.0 copy-start.6
  274.2 0.0 copy-start.8
  274.3 9.8 %fusion.9 = f32[2,32,24,2048]{3,2,1,0:T(8,128)} fusion(bf16[32,2,24,512]{3,2,0,1:T(8,128)(2,1)S(1)} %get-tuple-element.8, bf16[2,2048,512]{2,1,0:T(8,128)(2,1)} %param.13), kind=kOutput, calls=%fused_computation.15 | convolution fusion | flops 3221225472 | bytes 18350080 | tf_op jit(solution)/shard_map/nicf,idf->nicd/dot_general | solution.py:72
  284.0 0.0 copy-done.6
  284.0 7.7 %fusion = bf16[32,2,24,2048]{3,2,0,1:T(8,128)(2,1)S(1)} fusion(f32[2,32,24,2048]{3,2,1,0:T(8,128)} %fusion.9, bf16[32,2,24,512]{3,2,0,1:T(8,128)(2,1)S(1)} %get-tuple-element.7, bf16[2,2048,512]{2,1,0:T(8,128)(2,1)} %param.14), kind=kOutput, calls=%fused_computation.5 | convolution fusion | flops 3227516928 | bytes 24641536 | tf_op jit(solution)/shard_map/nicf,idf->nicd/dot_general | solution.py:73
  291.8 3.2 copy.62
  295.0 3.7 all-to-all-start
  298.8 0.1 convolution_convert_fusion.2
  299.0 0.2 fusion.43
  299.1 0.0 copy-start.7
  299.2 0.0 slice-start.1
  299.2 8.9 %bitcast_convert_fusion.1 = bf16[2,2048,512]{2,1,0:T(8,128)(2,1)} fusion(bf16[32,2,24,2048]{3,2,1,0:T(8,128)(2,1)} %bitcast.154, bf16[32,2,24,512]{3,2,0,1:T(8,128)(2,1)} %copy-done.8), kind=kOutput, calls=%fused_computation.3 | convolution fusion | flops 3223322624 | bytes 12058624 | tf_op jit(solution)/shard_map/nicd,nicf->idf/dot_general | solution.py:88
  308.0 0.0 copy-done.7
  308.0 9.4 %bitcast_convert_fusion.2 = bf16[2,2048,512]{2,1,0:T(8,128)(2,1)} fusion(bf16[32,2,24,2048]{3,2,1,0:T(8,128)(2,1)} %bitcast.155, bf16[32,2,24,512]{3,2,0,1:T(8,128)(2,1)S(1)} %copy-done.7), kind=kOutput, calls=%fused_computation.4 | convolution fusion | flops 3223322624 | bytes 12058624 | tf_op jit(solution)/shard_map/nicd,nicf->idf/dot_general | solution.py:85
  317.5 0.0 slice-done.1
  317.5 0.0 copy-start.2
  317.5 0.0 copy-start.10
  317.5 0.0 copy-start.12
  317.5 5.4 %bitcast_convert_fusion = bf16[2,512,2048]{2,1,0:T(8,128)(2,1)} fusion(bf16[32,2,24,2048]{3,2,1,0:T(8,128)(2,1)S(1)} %bitcast.151, f32[2,32,24,512]{3,2,1,0:T(8,128)S(1)} %copy-done.14, f32[2,32,24,512]{3,2,1,0:T(8,128)S(1)} %copy-done.13), kind=kOutput, calls=%fused_computation.2 | convolution fusion | flops 3228041216 | bytes 16777216 | tf_op jit(solution)/shard_map/nicf,nicd->ifd/dot_general | solution.py:82
  322.9 112.6 %all-to-all-done = bf16[32,48,2048]{2,1,0:T(8,128)(2,1)} async-done(((bf16[32,48,2048]{2,1,0:T(8,128)(2,1)}), bf16[32,48,2048]{2,1,0:T(8,128)(2,1)}, u32[]{:S(2)}, u32[]{:S(2)}) %all-to-all-start) | async-done | bytes 6291488 | tf_op jit(solution)/shard_map/all_to_all | solution.py:75
  435.5 0.0 copy-done.12
  435.5 0.0 copy-start.5
  435.5 4.1 fusion.39
  439.6 43.5 %psum.7 = f32[2048]{0:T(1024)S(1)} all-reduce(f32[2048]{0:T(1024)S(1)} %get-tuple-element.5), channel_id=1, replica_groups=mesh['dp'=8,'seq'=4] {'dp','seq'}, use_global_device_ids=true, to_apply=%region_7.8 | all-reduce | flops 2048 | bytes 16384 | tf_op jit(solution)/shard_map/psum | solution.py:107
  483.1 0.6 dynamic_slice.3
  483.7 1.2 fusion.46
  (21 shorter events, 0.2 us)
Async XLA Ops:
  7.2 161.5 %all-gather.10.cloned.1.call-start = ((), (), s32[]{:S(2)}) async-start(), calls=%async_computation.2 | async-start | bytes 17301504 | tf_op jit(solution)/shard_map/all_gather | solution.py:31
  8.4 10.6 %copy-start.11 = (f32[128]{0:T(128)}, f32[128]{0:T(128)S(1)}, u32[]{:S(2)}) copy-start(f32[128]{0:T(128)S(1)} %add_rsqrt_fusion) | copy-start | bytes 1540
  19.0 0.6 copy-start.9
  21.7 234.5 %all-gather.8.cloned.1.call-start = ((), (), s32[]{:S(2)}) async-start(), calls=%async_computation.1 | async-start | bytes 17301504 | tf_op jit(solution)/shard_map/all_gather | solution.py:25
  168.7 8.7 %copy-start.3 = (bf16[2,2048,512]{2,1,0:T(8,128)(2,1)S(1)}, bf16[2,2048,512]{2,1,0:T(8,128)(2,1)}, u32[]{:S(2)}) copy-start(bf16[2,2048,512]{2,1,0:T(8,128)(2,1)} %param.13) | copy-start | bytes 12582916
  177.4 5.2 %copy-start.1 = (bf16[32,48,2048]{2,1,0:T(8,128)(2,1)}, bf16[32,48,2048]{2,1,0:T(8,128)(2,1)S(1)}, u32[]{:S(2)}) copy-start(bf16[32,48,2048]{2,1,0:T(8,128)(2,1)S(1)} %convolution_convert_fusion) | copy-start | bytes 18874372
  177.4 5.1 %copy-start.4 = (bf16[2,2048,512]{2,1,0:T(8,128)(2,1)S(1)}, bf16[2,2048,512]{2,1,0:T(8,128)(2,1)}, u32[]{:S(2)}) copy-start(bf16[2,2048,512]{2,1,0:T(8,128)(2,1)} %param.14) | copy-start | bytes 12582916
  264.3 10.0 %copy-start = (bf16[32,48,2048]{2,1,0:T(8,128)(2,1)}, bf16[32,48,2048]{2,1,0:T(8,128)(2,1)S(1)}, u32[]{:S(2)}) copy-start(bf16[32,48,2048]{2,1,0:T(8,128)(2,1)S(1)} %multiply_convert_fusion) | copy-start | bytes 18874372
  274.2 9.8 %copy-start.6 = (bf16[32,2,24,512]{3,2,0,1:T(8,128)(2,1)}, bf16[32,2,24,512]{3,2,0,1:T(8,128)(2,1)S(1)}, u32[]{:S(2)}) copy-start(bf16[32,2,24,512]{3,2,0,1:T(8,128)(2,1)S(1)} %get-tuple-element.8) | copy-start | bytes 4718596
  274.2 9.8 %copy-start.8 = (bf16[32,2,24,512]{3,2,0,1:T(8,128)(2,1)}, bf16[32,2,24,512]{3,2,0,1:T(8,128)(2,1)S(1)}, u32[]{:S(2)}) copy-start(bf16[32,2,24,512]{3,2,0,1:T(8,128)(2,1)S(1)} %get-tuple-element.7) | copy-start | bytes 4718596
  295.0 22.4 %slice-start = ((s8[6291456]{0:T(1024)(128)(4,1)}), s8[2097152]{0:T(1024)(128)(4,1)S(1)}, s32[]{:S(2)}) async-start(s8[6291456]{0:T(1024)(128)(4,1)} %bitcast.149), calls=%async_computation.3 | async-start | bytes 4194304
  295.0 140.5 %all-to-all-start = ((bf16[32,48,2048]{2,1,0:T(8,128)(2,1)}), bf16[32,48,2048]{2,1,0:T(8,128)(2,1)}, u32[]{:S(2)}, u32[]{:S(2)}) async-start(bf16[32,48,2048]{2,1,0:T(8,128)(2,1)} %bitcast.147), calls=%async_computation | async-start | bytes 12582912 | tf_op jit(solution)/shard_map/all_to_all | solution.py:75
  299.1 8.9 %copy-start.7 = (bf16[32,2,24,512]{3,2,0,1:T(8,128)(2,1)S(1)}, bf16[32,2,24,512]{3,2,0,1:T(8,128)(2,1)}, u32[]{:S(2)}) copy-start(bf16[32,2,24,512]{3,2,0,1:T(8,128)(2,1)} %copy-done.6) | copy-start | bytes 4718596
  299.2 18.3 %slice-start.1 = ((s8[6291456]{0:T(1024)(128)(4,1)}), s8[4194304]{0:T(1024)(128)(4,1)S(1)}, s32[]{:S(2)}) async-start(s8[6291456]{0:T(1024)(128)(4,1)} %bitcast.149), calls=%async_computation.4 | async-start | bytes 8388608
  308.0 9.4 %copy-start.13 = (f32[2,32,24,512]{3,2,1,0:T(8,128)S(1)}, f32[2,32,24,512]{3,2,1,0:T(8,128)}, u32[]{:S(2)}) copy-start(f32[2,32,24,512]{3,2,1,0:T(8,128)} %fusion.1) | copy-start | bytes 9437188
  308.0 9.4 %copy-start.14 = (f32[2,32,24,512]{3,2,1,0:T(8,128)S(1)}, f32[2,32,24,512]{3,2,1,0:T(8,128)}, u32[]{:S(2)}) copy-start(f32[2,32,24,512]{3,2,1,0:T(8,128)} %fusion.3) | copy-start | bytes 9437188
  317.5 118.0 %copy-start.2 = (bf16[1,128,2048]{2,1,0:T(8,128)(2,1)S(1)}, bf16[1,128,2048]{2,1,0:T(8,128)(2,1)}, u32[]{:S(2)}) copy-start(bf16[1,128,2048]{2,1,0:T(8,128)(2,1)} %param.8) | copy-start | bytes 1572868
  317.5 118.0 %copy-start.10 = (f32[8,1,256]{2,1,0:T(1,128)S(1)}, f32[8,1,256]{2,1,0:T(1,128)}, u32[]{:S(2)}) copy-start(f32[8,1,256]{2,1,0:T(1,128)} %copy-done.9) | copy-start | bytes 24580
  317.5 118.0 %copy-start.12 = (f32[128]{0:T(128)S(1)}, f32[128]{0:T(128)}, u32[]{:S(2)}) copy-start(f32[128]{0:T(128)} %copy-done.11) | copy-start | bytes 1540
  435.5 48.2 %copy-start.5 = (bf16[1,128,2048]{2,1,0:T(8,128)(2,1)S(1)}, bf16[1,128,2048]{2,1,0:T(8,128)(2,1)}, u32[]{:S(2)}) copy-start(bf16[1,128,2048]{2,1,0:T(8,128)(2,1)} %param.9) | copy-start | bytes 1572868
Sparse Core Ops, SparseCore 0:
  21.8 117.1 all-gather.9
  142.0 114.1 all-gather.7
where the time goes:
time: 492 us
  blocking collectives  197 us (40%)
  waiting for transfers between devices  182 us (37%)
  matrix products  82.5 us (17%)
  between operations  14.3 us (3%)
  local copies, waits for them, and re-layouts  6.33 us (1%)
  other arithmetic  5.47 us (1%)
    all_to_all x1, waiting for transfers between devices, shards(): lax.all_to_all(returned.reshape(devices, local_experts * capacity, model_...  113 us
    all_gather x1, blocking collectives, shards(): lax.all_gather(weights_here.T, ('dp', 'seq'), axis=0, tiled=False)  74 us
    all_gather x1, blocking collectives, shards(): ids_all = lax.all_gather(ids_here.T, ('dp', 'seq'), axis=0, tiled=False)  69.5 us
    all_gather x1, waiting for transfers between devices, shards(): all_grads = lax.all_gather(upstream, ('dp', 'seq'), axis=0)  68.5 us
    psum x1, blocking collectives, shards(): total_gain = lax.psum(local_gain, ('dp', 'seq'))  43.5 us
    dot_general x2, matrix products, pick(): jnp.einsum('nst,ntd->nsd', picks, table, preferred_element_type=jnp.float32)  16.8 us
    all_gather x1, blocking collectives, shards(): gain_full = lax.all_gather(norm_gain, 'dp', axis=0, tiled=True)  10.6 us
    dot_general x1, matrix products, shards(): jnp.einsum('nicd,ifd->nicf', rows_grad, expert_down, preferred_element_ty...  9.94 us
  transfers between devices with their start and end apart: 3, of which 2 were waited for; matrix products, arithmetic and copies ran while one was open for 9% of the time, Pallas kernels for 0%

commit v1 on v0

--- a/solution.py
+++ b/solution.py
@@ -104,7 +104,7 @@
         preferred_element_type=jnp.float32,
     )
     local_gain = jnp.sum(summed * scaled, axis=0)
-    total_gain = lax.psum(local_gain, ("dp", "seq"))
+    total_gain = jnp.sum(lax.all_gather(local_gain, ("dp", "seq")), axis=0)
     shard_width = norm_gain.shape[0]
     grad_gain = lax.dynamic_slice(total_gain, (dp_at * shard_width,), (shard_width,))
     gained = summed * gain_full[None, :]

time: 492 us -> 518 us (1.053)
  blocking collectives: 197 us -> 223 us
    all_gather x0 -> x1, blocking collectives: none -> 69.4 us  [shards(): total_gain = jnp.sum(lax.all_gather(local_gain, ('dp', 'seq')), axis=0)]
    psum x1 -> x0, blocking collectives: 43.5 us -> none  [shards(): total_gain = lax.psum(local_gain, ('dp', 'seq'))]
where the time goes in v1:
time: 518 us
  blocking collectives  223 us (43%)
  waiting for transfers between devices  183 us (35%)
  matrix products  81 us (16%)
  between operations  14.3 us (3%)
  local copies, waits for them, and re-layouts  6.38 us (1%)
  other arithmetic  5.51 us (1%)
    all_to_all x1, waiting for transfers between devices, shards(): lax.all_to_all(returned.reshape(devices, local_experts * capacity, model_...  114 us
    all_gather x1, blocking collectives, shards(): lax.all_gather(weights_here.T, ('dp', 'seq'), axis=0, tiled=False)  74 us
    all_gather x1, blocking collectives, shards(): ids_all = lax.all_gather(ids_here.T, ('dp', 'seq'), axis=0, tiled=False)  69.5 us
    all_gather x1, blocking collectives, shards(): total_gain = jnp.sum(lax.all_gather(local_gain, ('dp', 'seq')), axis=0)  69.4 us
    all_gather x1, waiting for transfers between devices, shards(): all_grads = lax.all_gather(upstream, ('dp', 'seq'), axis=0)  68.5 us
    dot_general x2, matrix products, pick(): jnp.einsum('nst,ntd->nsd', picks, table, preferred_element_type=jnp.float32)  16.8 us
    all_gather x1, blocking collectives, shards(): gain_full = lax.all_gather(norm_gain, 'dp', axis=0, tiled=True)  10.6 us
  transfers between devices with their start and end apart: 3, of which 2 were waited for; matrix products, arithmetic and copies ran while one was open for 9% of the time, Pallas kernels for 0%

profile of v1, /device:TPU:0, one launch (start us, length us, event | category | flops | bytes accessed | tf_op | source)
XLA Modules:
  0.0 517.8 jit_solution(7038647929534936926)
XLA Ops:
  7.2 0.0 all-gather.11.cloned.1.call-start
  7.2 1.2 fusion.40
  8.5 10.6 %all-gather.5 = f32[8,1,256]{2,1,0:T(1,128)S(1)} all-gather(f32[1,1,256]{2,1,0:T(1,128)} %bitcast.166), channel_id=1, replica_groups=mesh['dp'=8,'seq'=4] {'dp'}, dimensions={0}, use_global_device_ids=true | all-gather | bytes 9216 | tf_op jit(solution)/shard_map/all_gather | solution.py:26
  19.0 0.0 copy-done.11
  19.0 0.6 copy-done.9
  19.6 2.0 fusion.42
  21.6 0.0 all-gather.11.cloned.1.call-update
  21.7 0.0 all-gather.9.cloned.1.call-start
  21.7 0.7 all-gather.9.cloned.1.call-update
  22.4 0.1 eq.88
  22.5 0.7 copy.91
  23.2 0.7 copy.92
  23.9 74.0 %all-gather.4 = f32[32,10,128]{2,1,0:T(8,128)S(1)} all-gather(f32[1,10,128]{2,1,0:T(8,128)S(1)} %bitcast.165), channel_id=3, replica_groups=mesh['dp'=8,'seq'=4] {'dp','seq'}, dimensions={0}, use_global_device_ids=true | all-gather | bytes 168960 | tf_op jit(solution)/shard_map/all_gather | solution.py:35
  97.8 0.1 copy.55
  97.9 69.5 %all-gather.3 = s32[32,10,128]{2,1,0:T(8,128)S(1)} all-gather(s32[1,10,128]{2,1,0:T(8,128)S(1)} %bitcast.163), channel_id=2, replica_groups=mesh['dp'=8,'seq'=4] {'dp','seq'}, dimensions={0}, use_global_device_ids=true | all-gather | bytes 168960 | tf_op jit(solution)/shard_map/all_gather | solution.py:34
  167.4 0.1 copy.52
  167.5 0.1 fusion.47
  167.6 0.1 compare_reduce_fusion
  167.7 0.1 convolution_convert_fusion.1
  167.9 0.4 select_reduce_fusion
  168.3 0.1 copy.57
  168.4 0.1 copy.58
  168.4 0.2 fusion.45
  168.7 0.0 all-gather.11.cloned.1.call-done
  168.7 0.0 copy-start.3
  168.7 8.7 %convolution_convert_fusion = bf16[32,48,2048]{2,1,0:T(8,128)(2,1)S(1)} fusion(pred[32,48,128]{2,1,0:T(8,128)(4,1)S(1)} %fusion.45, bf16[32,128,2048]{2,1,0:T(8,128)(2,1)} %all-gather.11.cloned.1.call-done), kind=kOutput, calls=%fused_computation.14 | convolution fusion | flops 808452096 | bytes 23265280 | tf_op jit(solution)/shard_map/nst,ntd->nsd/dot_general | solution.py:52
  177.4 0.0 copy-start.1
  177.4 0.0 copy-done.3
  177.4 0.0 copy-start.4
  177.4 5.1 fusion.1
  182.5 0.0 copy-done.1
  182.5 0.0 copy-done.4
  182.5 5.1 fusion.3
  187.7 68.5 %all-gather.9.cloned.1.call-done = bf16[32,128,2048]{2,1,0:T(8,128)(2,1)} async-done(((bf16[1,128,2048]{2,1,0:T(8,128)(2,1)}), bf16[32,128,2048]{2,1,0:T(8,128)(2,1)}) %all-gather.9.cloned.1.call-update) | async-done | bytes 16777232 | tf_op jit(solution)/shard_map/all_gather | solution.py:25
  256.2 8.1 %multiply_convert_fusion = bf16[32,48,2048]{2,1,0:T(8,128)(2,1)S(1)} fusion(f32[32,48]{1,0:T(8,128)S(1)} %copy.58, pred[32,48,128]{2,1,0:T(8,128)(4,1)S(1)} %fusion.45, bf16[32,128,2048]{2,1,0:T(8,128)(2,1)} %all-gather.9.cloned.1.call-done), kind=kOutput, calls=%fused_computation.1 | convolution fusion | flops 811597824 | bytes 23271424 | tf_op jit(solution)/shard_map/nst,ntd->nsd/dot_general | solution.py:52
  264.3 0.0 copy-start
  264.3 9.9 %fusion.25 = (bf16[32,2,24,512]{3,2,0,1:T(8,128)(2,1)S(1)}, bf16[32,2,24,512]{3,2,0,1:T(8,128)(2,1)S(1)}) fusion(f32[2,32,24,512]{3,2,1,0:T(8,128)} %fusion.1, f32[2,32,24,512]{3,2,1,0:T(8,128)} %fusion.3, bf16[2,512,2048]{2,1,0:T(8,128)(2,1)} %param.15, bf16[32,2,24,2048]{3,2,1,0:T(8,128)(2,1)S(1)} %bitcast.148), kind=kOutput, calls=%fused_computation.35 | convolution fusion | flops 3231449088 | bytes 19922944 | tf_op jit(solution)/shard_map/nicd,ifd->nicf/dot_general | solution.py:57
  274.2 0.0 copy-done
  274.2 0.0 copy-start.6
  274.2 0.0 copy-start.8
  274.3 9.8 %fusion.9 = f32[2,32,24,2048]{3,2,1,0:T(8,128)} fusion(bf16[32,2,24,512]{3,2,0,1:T(8,128)(2,1)S(1)} %get-tuple-element.8, bf16[2,2048,512]{2,1,0:T(8,128)(2,1)} %param.13), kind=kOutput, calls=%fused_computation.15 | convolution fusion | flops 3221225472 | bytes 18350080 | tf_op jit(solution)/shard_map/nicf,idf->nicd/dot_general | solution.py:72
  284.0 0.0 copy-done.6
  284.0 0.0 copy-done.8
  284.0 7.7 %fusion = bf16[32,2,24,2048]{3,2,0,1:T(8,128)(2,1)S(1)} fusion(f32[2,32,24,2048]{3,2,1,0:T(8,128)} %fusion.9, bf16[32,2,24,512]{3,2,0,1:T(8,128)(2,1)S(1)} %get-tuple-element.7, bf16[2,2048,512]{2,1,0:T(8,128)(2,1)} %param.14), kind=kOutput, calls=%fused_computation.5 | convolution fusion | flops 3227516928 | bytes 24641536 | tf_op jit(solution)/shard_map/nicf,idf->nicd/dot_general | solution.py:73
  291.8 3.2 copy.62
  295.0 3.7 all-to-all-start
  298.8 0.1 convolution_convert_fusion.2
  298.9 0.2 fusion.43
  299.1 0.0 slice-start.3
  299.1 0.0 copy-start.7
  299.1 0.0 slice-start
  299.1 8.9 %bitcast_convert_fusion.1 = bf16[2,2048,512]{2,1,0:T(8,128)(2,1)} fusion(bf16[32,2,24,2048]{3,2,1,0:T(8,128)(2,1)} %bitcast.154, bf16[32,2,24,512]{3,2,0,1:T(8,128)(2,1)} %copy-done.8), kind=kOutput, calls=%fused_computation.3 | convolution fusion | flops 3223322624 | bytes 12058624 | tf_op jit(solution)/shard_map/nicd,nicf->idf/dot_general | solution.py:88
  308.0 0.0 slice-start.1
  308.0 5.1 bitcast_convert_fusion.2
  313.1 0.0 slice-done.1
  313.1 0.0 copy-start.12
  313.1 8.3 %bitcast_convert_fusion = bf16[2,512,2048]{2,1,0:T(8,128)(2,1)} fusion(bf16[32,2,24,2048]{3,2,1,0:T(8,128)(2,1)S(1)} %bitcast.151, f32[2,32,24,512]{3,2,1,0:T(8,128)} %fusion.3, f32[2,32,24,512]{3,2,1,0:T(8,128)} %fusion.1), kind=kOutput, calls=%fused_computation.2 | convolution fusion | flops 3228041216 | bytes 16777216 | tf_op jit(solution)/shard_map/nicf,nicd->ifd/dot_general | solution.py:82
  321.4 114.0 %all-to-all-done = bf16[32,48,2048]{2,1,0:T(8,128)(2,1)} async-done(((bf16[32,48,2048]{2,1,0:T(8,128)(2,1)}), bf16[32,48,2048]{2,1,0:T(8,128)(2,1)}, u32[]{:S(2)}, u32[]{:S(2)}) %all-to-all-start) | async-done | bytes 6291488 | tf_op jit(solution)/shard_map/all_to_all | solution.py:75
  435.5 0.0 copy-done.10
  435.5 0.0 copy-start.5
  435.5 4.1 fusion.39
  439.6 69.4 %all-gather.2 = f32[65536]{0:T(1024)S(1)} all-gather(f32[2048]{0:T(1024)S(1)} %get-tuple-element.5), channel_id=4, replica_groups=mesh['dp'=8,'seq'=4] {'dp','seq'}, dimensions={0}, use_global_device_ids=true | all-gather | bytes 270336 | tf_op jit(solution)/shard_map/all_gather | solution.py:107
  509.1 1.2 fusion.46
  510.3 0.6 dynamic_slice.3
  (24 shorter events, 0.2 us)
Async XLA Ops:
  7.2 161.5 %all-gather.11.cloned.1.call-start = ((), (), s32[]{:S(2)}) async-start(), calls=%async_computation.2 | async-start | bytes 17301504 | tf_op jit(solution)/shard_map/all_gather | solution.py:31
  8.4 10.6 %copy-start.11 = (f32[128]{0:T(128)}, f32[128]{0:T(128)S(1)}, u32[]{:S(2)}) copy-start(f32[128]{0:T(128)S(1)} %add_rsqrt_fusion) | copy-start | bytes 1540
  19.0 0.6 copy-start.9
  21.7 234.5 %all-gather.9.cloned.1.call-start = ((), (), s32[]{:S(2)}) async-start(), calls=%async_computation.1 | async-start | bytes 17301504 | tf_op jit(solution)/shard_map/all_gather | solution.py:25
  168.7 8.7 %copy-start.3 = (bf16[2,2048,512]{2,1,0:T(8,128)(2,1)S(1)}, bf16[2,2048,512]{2,1,0:T(8,128)(2,1)}, u32[]{:S(2)}) copy-start(bf16[2,2048,512]{2,1,0:T(8,128)(2,1)} %param.13) | copy-start | bytes 12582916
  177.4 5.1 copy-start.1
  177.4 5.1 copy-start.4
  264.3 10.0 %copy-start = (bf16[32,48,2048]{2,1,0:T(8,128)(2,1)}, bf16[32,48,2048]{2,1,0:T(8,128)(2,1)S(1)}, u32[]{:S(2)}) copy-start(bf16[32,48,2048]{2,1,0:T(8,128)(2,1)S(1)} %multiply_convert_fusion) | copy-start | bytes 18874372
  274.2 9.8 %copy-start.6 = (bf16[32,2,24,512]{3,2,0,1:T(8,128)(2,1)}, bf16[32,2,24,512]{3,2,0,1:T(8,128)(2,1)S(1)}, u32[]{:S(2)}) copy-start(bf16[32,2,24,512]{3,2,0,1:T(8,128)(2,1)S(1)} %get-tuple-element.8) | copy-start | bytes 4718596
  274.2 9.8 %copy-start.8 = (bf16[32,2,24,512]{3,2,0,1:T(8,128)(2,1)}, bf16[32,2,24,512]{3,2,0,1:T(8,128)(2,1)S(1)}, u32[]{:S(2)}) copy-start(bf16[32,2,24,512]{3,2,0,1:T(8,128)(2,1)S(1)} %get-tuple-element.7) | copy-start | bytes 4718596
  295.0 13.0 %slice-start.2 = ((s8[6291456]{0:T(1024)(128)(4,1)}), s8[2097152]{0:T(1024)(128)(4,1)S(1)}, s32[]{:S(2)}) async-start(s8[6291456]{0:T(1024)(128)(4,1)} %bitcast.155), calls=%async_computation.5 | async-start | bytes 4194304
  295.0 140.5 %all-to-all-start = ((bf16[32,48,2048]{2,1,0:T(8,128)(2,1)}), bf16[32,48,2048]{2,1,0:T(8,128)(2,1)}, u32[]{:S(2)}, u32[]{:S(2)}) async-start(bf16[32,48,2048]{2,1,0:T(8,128)(2,1)} %bitcast.147), calls=%async_computation | async-start | bytes 12582912 | tf_op jit(solution)/shard_map/all_to_all | solution.py:75
  299.1 8.9 %slice-start.3 = ((s8[6291456]{0:T(1024)(128)(4,1)}), s8[4194304]{0:T(1024)(128)(4,1)S(1)}, s32[]{:S(2)}) async-start(s8[6291456]{0:T(1024)(128)(4,1)} %bitcast.155), calls=%async_computation.6 | async-start | bytes 8388608
  299.1 8.9 %copy-start.7 = (bf16[32,2,24,512]{3,2,0,1:T(8,128)(2,1)S(1)}, bf16[32,2,24,512]{3,2,0,1:T(8,128)(2,1)}, u32[]{:S(2)}) copy-start(bf16[32,2,24,512]{3,2,0,1:T(8,128)(2,1)} %copy-done.6) | copy-start | bytes 4718596
  299.1 14.0 %slice-start = ((s8[6291456]{0:T(1024)(128)(4,1)}), s8[4194304]{0:T(1024)(128)(4,1)S(1)}, s32[]{:S(2)}) async-start(s8[6291456]{0:T(1024)(128)(4,1)} %bitcast.149), calls=%async_computation.3 | async-start | bytes 8388608
  308.0 5.1 slice-start.1
  313.1 122.4 %copy-start.2 = (bf16[1,128,2048]{2,1,0:T(8,128)(2,1)S(1)}, bf16[1,128,2048]{2,1,0:T(8,128)(2,1)}, u32[]{:S(2)}) copy-start(bf16[1,128,2048]{2,1,0:T(8,128)(2,1)} %param.8) | copy-start | bytes 1572868
  313.1 122.4 %copy-start.10 = (f32[8,1,256]{2,1,0:T(1,128)S(1)}, f32[8,1,256]{2,1,0:T(1,128)}, u32[]{:S(2)}) copy-start(f32[8,1,256]{2,1,0:T(1,128)} %copy-done.9) | copy-start | bytes 24580
  313.1 122.4 %copy-start.12 = (f32[128]{0:T(128)S(1)}, f32[128]{0:T(128)}, u32[]{:S(2)}) copy-start(f32[128]{0:T(128)} %copy-done.11) | copy-start | bytes 1540
  435.5 73.6 %copy-start.5 = (bf16[1,128,2048]{2,1,0:T(8,128)(2,1)S(1)}, bf16[1,128,2048]{2,1,0:T(8,128)(2,1)}, u32[]{:S(2)}) copy-start(bf16[1,128,2048]{2,1,0:T(8,128)(2,1)} %param.9) | copy-start | bytes 1572868
Sparse Core Ops, SparseCore 0:
  21.8 117.1 all-gather.10
  142.0 114.1 all-gather.8
